TPU v7x, 32 devices: a whole 2x2x4 slice. The times are simulated.
32 devices in a mesh: groups: 2 (over x), tm: 4 (over y, core), rows: 4 (over z).
Axes of the slice: x: 2, y: 2, z: 4, core: 2. Of those that a mesh axis runs over, the one named last changes fastest.
Arguments:
- features: bfloat16 [16, 8, 96, 512], P(('groups', 'tm'), 'rows'), parts along dimension 0, may hold values from -6 to 6
- spatial_weight: bfloat16 [3, 3, 512, 512], replicated, may hold values from -0.09375 to 0.09375
- temporal_weight: bfloat16 [3, 512, 512], replicated, may hold values from -0.15625 to 0.15625
- head_weight: bfloat16 [512, 16], replicated, may hold values from -0.25 to 0.25
- embed_weight: bfloat16 [64, 5120], replicated, may hold values from -0.75 to 0.75
- ada_scale: bfloat16 [5120], replicated, may hold values from -0.5 to 0.5
- ada_shift: bfloat16 [5120], replicated, may hold values from -3 to 3
- qkv_weight: bfloat16 [5120, 9216], P('tm', 'rows'), may hold values from -0.078125 to 0.078125
Outputs:
- qkv: float32 [3072, 9216], P(('groups', 'tm'), 'rows'), parts along dimension 0
There are 2 independent parts, one for each index of `groups`. A program takes and returns all parts, laid end to end along the dimension named above; an argument that names none is the same for every part. Nothing has to cross between parts.
All inputs are finite; a program needn't handle non-finite values.
Results may differ from a plain program's by a relative error of at most 0.0056.
Values may be sent and summed in bfloat16 or wider, within the bound.
A program may use at most 128 MiB of HBM per device.

v0:
```python
import jax
import jax.numpy as jnp
from jax import lax
from jax.sharding import PartitionSpec as P

LATENT = 16
PATCH = 2
PDIM = 64


def with_halo(cells, sides, width):
    for axis, dim in sides:
        count = lax.axis_size(axis)
        ends = count - 1
        head = lax.slice_in_dim(cells, 0, width, axis=dim)
        tail = lax.slice_in_dim(cells, cells.shape[dim] - width, cells.shape[dim], axis=dim)
        cells = jnp.concatenate(
            [
                lax.ppermute(tail, axis, [(i, (i + 1) % count) for i in range(ends)]),
                cells,
                lax.ppermute(head, axis, [((i + 1) % count, i) for i in range(ends)]),
            ],
            axis=dim,
        )
    return cells


def passed_along(block, axis, distance):
    devices = range(lax.axis_size(axis))
    route = [(i - distance, i) for i in devices if i - distance in devices]
    return lax.ppermute(block, axis, route)


def norm_silu(values):
    scaled = values * lax.rsqrt(jnp.mean(values * values, axis=-1, keepdims=True) + 1e-06)
    return jax.nn.silu(scaled)


def per_device(
    features,
    spatial_weight,
    temporal_weight,
    head_weight,
    embed_weight,
    ada_scale,
    ada_shift,
    qkv_weight,
):
    frames_dev, rows_dev, columns, channels = features.shape
    activated = norm_silu(features.astype(jnp.float32)).astype(jnp.bfloat16)
    rimmed = with_halo(activated, (("rows", 1),), 1)
    padded = jnp.pad(rimmed, ((0, 0), (0, 0), (1, 1), (0, 0)))
    spatial = jnp.zeros((frames_dev * rows_dev * columns, channels), jnp.float32)
    for tap_row in range(3):
        for tap_col in range(3):
            window = padded[:, tap_row : tap_row + rows_dev, tap_col : tap_col + columns].reshape(
                -1, channels
            )
            spatial = spatial + jnp.dot(
                window, spatial_weight[tap_row, tap_col], preferred_element_type=jnp.float32
            )
    mixed_act = (
        norm_silu(spatial).astype(jnp.bfloat16).reshape(frames_dev, rows_dev, columns, channels)
    )
    before = passed_along(mixed_act, "tm", 1)
    stacked = jnp.concatenate([before, mixed_act], axis=0)
    temporal = jnp.zeros((frames_dev * rows_dev * columns, channels), jnp.float32)
    for tap in range(3):
        temporal = temporal + jnp.dot(
            stacked[tap : tap + frames_dev].reshape(-1, channels),
            temporal_weight[tap],
            preferred_element_type=jnp.float32,
        )
    summed = features.astype(jnp.float32).reshape(-1, channels) + temporal
    latent = jnp.dot(
        norm_silu(summed).astype(jnp.bfloat16), head_weight, preferred_element_type=jnp.float32
    ).astype(jnp.bfloat16)
    latent = latent.reshape(frames_dev, 1, PATCH, columns // PATCH, PATCH, LATENT)
    patches = jnp.transpose(latent, (0, 1, 3, 2, 4, 5)).reshape(
        frames_dev, 1, columns // PATCH, PDIM
    )
    token_block = lax.all_gather(patches, "rows", axis=1, tiled=True)
    block_rows = token_block.shape[0] * token_block.shape[1] * token_block.shape[2]
    embedded = jnp.dot(
        token_block.reshape(block_rows, PDIM), embed_weight, preferred_element_type=jnp.float32
    ).astype(jnp.bfloat16)
    widened = lax.optimization_barrier(embedded).astype(jnp.float32)
    centered = widened - jnp.mean(widened, axis=-1, keepdims=True)
    spread = jnp.mean(centered * centered, axis=-1, keepdims=True)
    modulated = centered * lax.rsqrt(spread + 1e-06) * (
        1.0 + ada_scale.astype(jnp.float32)
    ) + ada_shift.astype(jnp.float32)
    normalized = modulated.astype(jnp.bfloat16)
    whole_columns = lax.all_gather(qkv_weight, "tm", axis=0, tiled=True)
    projected = jnp.dot(normalized, whole_columns, preferred_element_type=jnp.float32)
    return projected


def solution(mesh):
    return jax.shard_map(
        per_device,
        mesh=mesh,
        in_specs=(
            P(("groups", "tm"), "rows", None, None),
            P(),
            P(),
            P(),
            P(),
            P(),
            P(),
            P("tm", "rows"),
        ),
        out_specs=P(("groups", "tm"), "rows"),
        check_vma=False,
    )
```

profile of v0, /device:TPU:0, one launch (start us, length us, event | category | flops | bytes accessed | tf_op | source)
XLA Modules:
  0.0 182.8 jit_solution(10699574002116954827)
XLA Ops:
  6.6 0.7 all-gather.2.cloned.1.call-update
  8.1 5.0 %collective-permute-start = (bf16[2,1,96,512]{3,2,1,0:T(8,128)(2,1)S(1)}, bf16[2,1,96,512]{3,2,1,0:T(8,128)(2,1)S(1)}, u32[]{:S(2)}, u32[]{:S(2)}) collective-permute-start(bf16[2,1,96,512]{3,2,1,0:T(8,128)(2,1)S(1)} %get-tuple-element.13), channel_id=1, source_target_pairs={{0,1},{1,2},{2,3},{4,5},{5,6},{6,7},{8,9},{9,10},{10,11},{12,13},{... | collective-permute-start | bytes 589832 | tf_op jit(solution)/shard_map/ppermute | solution.py:19
  13.1 1.3 collective-permute-start.1
  14.4 2.8 %collective-permute-done = bf16[2,1,96,512]{3,2,1,0:T(8,128)(2,1)S(1)} collective-permute-done((bf16[2,1,96,512]{3,2,1,0:T(8,128)(2,1)S(1)}, bf16[2,1,96,512]{3,2,1,0:T(8,128)(2,1)S(1)}, u32[]{:S(2)}, u32[]{:S(2)}) %collective-permute-start) | collective-permute-done | bytes 196640 | tf_op jit(solution)/shard_map/ppermute | solution.py:19
  17.2 4.1 %collective-permute-done.1 = bf16[2,1,96,512]{3,2,1,0:T(8,128)(2,1)S(1)} collective-permute-done((bf16[2,1,96,512]{3,2,1,0:T(8,128)(2,1)S(1)}, bf16[2,1,96,512]{3,2,1,0:T(8,128)(2,1)S(1)}, u32[]{:S(2)}, u32[]{:S(2)}) %collective-permute-start.1) | collective-permute-done | bytes 196640 | tf_op jit(solution)/shard_map/ppermute | solution.py:21
  22.7 0.4 convolution_add_fusion.7
  23.1 0.4 convolution_add_fusion.6
  23.5 0.4 convolution_add_fusion.5
  23.9 0.4 convolution_add_fusion.4
  24.3 0.4 convolution_add_fusion.3
  24.6 0.4 convolution_add_fusion.2
  25.0 0.5 multiply_reduce_fusion.1
  25.8 1.3 collective-permute-start.2
  27.5 1.5 collective-permute-done.2
  29.0 0.4 fusion.23
  29.4 0.5 multiply_reduce_fusion
  29.9 0.4 convolution_convert_fusion.1
  30.7 13.6 %all_gather.6 = bf16[2,4,48,64]{3,2,0,1:T(8,128)(2,1)S(1)} all-gather(bf16[2,1,48,64]{3,2,0,1:T(8,128)(2,1)S(1)} %copy.16), channel_id=1, replica_groups=mesh['groups'=2,'tm'=4,'rows'=4] {'rows'}, dimensions={1}, use_global_device_ids=true | all-gather | bytes 61440 | tf_op jit(solution)/shard_map/all_gather | solution.py:82
  44.6 1.2 convolution_convert_fusion
  45.9 0.6 convert_reduce_fusion
  46.5 1.4 copy-done.1
  47.8 1.2 fusion.2
  49.0 108.7 %all-gather.2.cloned.1.call-done = bf16[5120,2304]{1,0:T(8,128)(2,1)} async-done(((bf16[1280,2304]{1,0:T(8,128)(2,1)}), bf16[5120,2304]{1,0:T(8,128)(2,1)}) %all-gather.2.cloned.1.call-update) | async-done | bytes 23592976 | tf_op jit(solution)/shard_map/all_gather | solution.py:94
  157.8 18.2 %fusion.6 = f32[384,2304]{1,0:T(8,128)} fusion(bf16[5120,2304]{1,0:T(8,128)(2,1)} %all-gather.2.cloned.1.call-done, bf16[384,5120]{1,0:T(8,128)(2,1)} %copy-done.1, f32[5120]{0:T(1024)S(1)} %convert_element_type.41, f32[5120]{0:T(1024)S(1)} %convert_add_fusion, f32[384]{0:T(512)S(1)} %add_rsqrt_fusion, f32[384]{0:T(512)S(1)} %broadcast_multiply_fusion), kind=kOutput, calls=%fused_computation.9 | convolution fusion | flops 9071493120 | bytes 31108096 | tf_op jit(solution)/shard_map/dot_general | solution.py:95
  (42 shorter events, 3.6 us)
Async XLA Ops:
  6.5 38.1 %copy-start = (bf16[64,5120]{1,0:T(8,128)(2,1)S(1)}, bf16[64,5120]{1,0:T(8,128)(2,1)}, u32[]{:S(2)}) copy-start(bf16[64,5120]{1,0:T(8,128)(2,1)} %param.12) | copy-start | bytes 1966084
  6.5 1.1 copy-start.2
  6.5 7.9 %copy-start.4 = (bf16[5120]{0:T(1024)(128)(2,1)S(1)}, bf16[5120]{0:T(1024)(128)(2,1)}, u32[]{:S(2)}) copy-start(bf16[5120]{0:T(1024)(128)(2,1)} %param.14) | copy-start | bytes 30724
  6.5 151.2 %all-gather.2.cloned.1.call-start = ((), (), s32[]{:S(2)}) async-start(), calls=%async_computation | async-start | bytes 29491200 | tf_op jit(solution)/shard_map/all_gather | solution.py:94
  6.5 15.4 %slice-start = ((s8[4718592]{0:T(1024)(128)(4,1)}), s8[524288]{0:T(1024)(128)(4,1)S(1)}, s32[]{:S(2)}) async-start(s8[4718592]{0:T(1024)(128)(4,1)} %bitcast.77), calls=%async_computation.1 | async-start | bytes 1048576
  8.1 9.1 %collective-permute-start = (bf16[2,1,96,512]{3,2,1,0:T(8,128)(2,1)S(1)}, bf16[2,1,96,512]{3,2,1,0:T(8,128)(2,1)S(1)}, u32[]{:S(2)}, u32[]{:S(2)}) collective-permute-start(bf16[2,1,96,512]{3,2,1,0:T(8,128)(2,1)S(1)} %get-tuple-element.13), channel_id=1, source_target_pairs={{0,1},{1,2},{2,3},{4,5},{5,6},{6,7},{8,9},{9,10},{10,11},{12,13},{... | collective-permute-start | bytes 589832 | tf_op jit(solution)/shard_map/ppermute | solution.py:19
  13.1 8.3 %collective-permute-start.1 = (bf16[2,1,96,512]{3,2,1,0:T(8,128)(2,1)S(1)}, bf16[2,1,96,512]{3,2,1,0:T(8,128)(2,1)S(1)}, u32[]{:S(2)}, u32[]{:S(2)}) collective-permute-start(bf16[2,1,96,512]{3,2,1,0:T(8,128)(2,1)S(1)} %get-tuple-element.14), channel_id=1, source_target_pairs={{1,0},{2,1},{3,2},{5,4},{6,5},{7,6},{9,8},{10,9},{11,10},{13,12},{... | collective-permute-start | bytes 589832 | tf_op jit(solution)/shard_map/ppermute | solution.py:21
  14.4 7.6 %slice-start.1 = ((s8[4718592]{0:T(1024)(128)(4,1)}), s8[4194304]{0:T(1024)(128)(4,1)S(1)}, s32[]{:S(2)}) async-start(s8[4718592]{0:T(1024)(128)(4,1)} %bitcast.77), calls=%async_computation.2 | async-start | bytes 8388608
  24.2 2.9 %copy-start.5 = (bf16[5120]{0:T(1024)(128)(2,1)S(1)}, bf16[5120]{0:T(1024)(128)(2,1)}, u32[]{:S(2)}) copy-start(bf16[5120]{0:T(1024)(128)(2,1)} %param.13) | copy-start | bytes 30724
  24.3 2.9 %copy-start.3 = (bf16[3,512,512]{2,1,0:T(8,128)(2,1)S(1)}, bf16[3,512,512]{2,1,0:T(8,128)(2,1)}, u32[]{:S(2)}) copy-start(bf16[3,512,512]{2,1,0:T(8,128)(2,1)} %param.10) | copy-start | bytes 4718596
  25.5 4.4 %copy-start.6 = (bf16[512,16]{0,1:T(8,128)(2,1)S(1)}, bf16[512,16]{0,1:T(8,128)(2,1)}, u32[]{:S(2)}) copy-start(bf16[512,16]{0,1:T(8,128)(2,1)} %param.11) | copy-start | bytes 49156
  25.8 3.2 %collective-permute-start.2 = (bf16[2,2,96,512]{3,2,1,0:T(8,128)(2,1)S(1)}, bf16[2,2,96,512]{3,2,1,0:T(8,128)(2,1)S(1)}, u32[]{:S(2)}, u32[]{:S(2)}) collective-permute-start(bf16[2,2,96,512]{3,2,1,0:T(8,128)(2,1)S(1)} %bitcast.80), channel_id=1, source_target_pairs={{0,4},{4,8},{8,12},{1,5},{5,9},{9,13},{2,6},{6,10},{10,14},{3,7},{... | collective-permute-start | bytes 1179656 | tf_op jit(solution)/shard_map/ppermute | solution.py:31
  45.8 2.0 %copy-start.1 = (bf16[384,5120]{1,0:T(8,128)(2,1)}, bf16[384,5120]{1,0:T(8,128)(2,1)S(1)}, u32[]{:S(2)}) copy-start(bf16[384,5120]{1,0:T(8,128)(2,1)S(1)} %convolution_convert_fusion) | copy-start | bytes 11796484
Sparse Core Ops, SparseCore 0:
  8.9 148.7 all-gather.1
where the time goes:
time: 185 us; the launch traced here: 183 us
  waiting for transfers between devices  118 us (64%)
  matrix products  24.4 us (13%)
  between operations  13.7 us (7%)
  blocking collectives  13.6 us (7%)
  starting transfers between devices  7.58 us (4%)
  other arithmetic  2.89 us (2%)
  local copies, waits for them, and re-layouts  2.73 us (1%)
    all_gather x1, waiting for transfers between devices, per_device(): whole_columns = lax.all_gather(qkv_weight, 'tm', axis=0, tiled=True)  109 us
    dot_general x1, matrix products, per_device(): jnp.dot(normalized, whole_columns, preferred_element_type=jnp.float32)  18.2 us
    all_gather x1, blocking collectives, per_device(): token_block = lax.all_gather(patches, 'rows', axis=1, tiled=True)  13.6 us
    ppermute x1, starting transfers between devices, with_halo(): lax.ppermute(tail, axis, [(i, (i + 1) % count) for i in range(ends)])  4.97 us
    ppermute x1, waiting for transfers between devices, with_halo(): lax.ppermute(head, axis, [((i + 1) % count, i) for i in range(ends)])  4.12 us
  transfers between devices with their start and end apart: 4, of which 4 were waited for; matrix products, arithmetic and copies ran while one was open for 6% of the time, Pallas kernels for 0%

commit v1 on v0

--- a/solution.py
+++ b/solution.py
@@ -31,6 +31,22 @@
     return lax.ppermute(block, axis, route)
 
 
+def halves(values):
+    high = lax.reduce_precision(values, 8, 7)
+    return high.astype(jnp.bfloat16), (values - high).astype(jnp.bfloat16)
+
+
+def summed_over(values, axis):
+    count = lax.axis_size(axis)
+    if count & (count - 1):
+        return lax.psum(values, axis)
+    step = 1
+    while step < count:
+        values = values + lax.ppermute(values, axis, [(i, i ^ step) for i in range(count)])
+        step *= 2
+    return values
+
+
 def norm_silu(values):
     scaled = values * lax.rsqrt(jnp.mean(values * values, axis=-1, keepdims=True) + 1e-06)
     return jax.nn.silu(scaled)
@@ -47,6 +63,25 @@
     qkv_weight,
 ):
     frames_dev, rows_dev, columns, channels = features.shape
+    depth = qkv_weight.shape[0]
+    start = lax.axis_index("tm") * depth
+    wide = embed_weight.astype(jnp.float32)
+    wide = wide - jnp.mean(wide, axis=1, keepdims=True)
+    gram = lax.dot_general(
+        wide, wide, (((1,), (1,)), ((), ())), precision=lax.Precision.HIGHEST
+    ) / wide.shape[1]
+    scaled = lax.dynamic_slice_in_dim(
+        wide * (1.0 + ada_scale.astype(jnp.float32)), start, depth, axis=1
+    )
+    shift = lax.dynamic_slice_in_dim(ada_shift, start, depth, axis=0)
+    terms = jnp.dot(
+        jnp.concatenate([*halves(scaled), shift[None]], axis=0),
+        qkv_weight,
+        preferred_element_type=jnp.float32,
+    )
+    folded = summed_over(
+        jnp.concatenate([terms[:PDIM] + terms[PDIM : 2 * PDIM], terms[2 * PDIM :]], axis=0), "tm"
+    )
     activated = norm_silu(features.astype(jnp.float32)).astype(jnp.bfloat16)
     rimmed = with_halo(activated, (("rows", 1),), 1)
     padded = jnp.pad(rimmed, ((0, 0), (0, 0), (1, 1), (0, 0)))
@@ -81,18 +116,17 @@
     )
     token_block = lax.all_gather(patches, "rows", axis=1, tiled=True)
     block_rows = token_block.shape[0] * token_block.shape[1] * token_block.shape[2]
-    embedded = jnp.dot(
-        token_block.reshape(block_rows, PDIM), embed_weight, preferred_element_type=jnp.float32
-    ).astype(jnp.bfloat16)
-    widened = lax.optimization_barrier(embedded).astype(jnp.float32)
-    centered = widened - jnp.mean(widened, axis=-1, keepdims=True)
-    spread = jnp.mean(centered * centered, axis=-1, keepdims=True)
-    modulated = centered * lax.rsqrt(spread + 1e-06) * (
-        1.0 + ada_scale.astype(jnp.float32)
-    ) + ada_shift.astype(jnp.float32)
-    normalized = modulated.astype(jnp.bfloat16)
-    whole_columns = lax.all_gather(qkv_weight, "tm", axis=0, tiled=True)
-    projected = jnp.dot(normalized, whole_columns, preferred_element_type=jnp.float32)
+    block = token_block.reshape(block_rows, PDIM)
+    moment = jnp.dot(
+        block.astype(jnp.float32), gram, precision=lax.Precision.HIGHEST
+    ) * block.astype(jnp.float32)
+    spread = jnp.maximum(jnp.sum(moment, axis=-1, keepdims=True), 0.0)
+    product = jnp.dot(
+        jnp.concatenate([block, block], axis=1),
+        jnp.concatenate(halves(folded[:PDIM]), axis=0),
+        preferred_element_type=jnp.float32,
+    )
+    projected = product * lax.rsqrt(spread + 1e-06) + folded[PDIM : PDIM + 1]
     return projected
 
 

time: 185 us -> 49.8 us (0.27); the launches traced: 183 us -> 49.5 us
  waiting for transfers between devices: 118 us -> 1.57 us
  between operations: 13.7 us -> 0.39 us
  matrix products: 24.4 us -> 12.9 us
  starting transfers between devices: 7.58 us -> 14.8 us
    all_gather x1 -> x0, waiting for transfers between devices: 109 us -> none  [per_device(): whole_columns = lax.all_gather(qkv_weight, 'tm', axis=0, tiled=True)]
    dot_general x2 -> x4, matrix products: 19.4 us -> 7.93 us  [the longest x1 3.81 us: per_device(): jnp.dot(jnp.concatenate([*halves(scaled), shift[None]], axis=0), qkv_weig...]
    ppermute x0 -> x2, starting transfers between devices: none -> 7.07 us  [summed_over(): lax.ppermute(values, axis, [(i, i ^ step) for i in range(count)])]
    ppermute x1, waiting for transfers between devices: 2.79 us -> 0.01 us  [with_halo(): lax.ppermute(tail, axis, [(i, (i + 1) % count) for i in range(ends)])]
    ppermute x1, waiting for transfers between devices: 4.12 us -> 1.56 us  [with_halo(): lax.ppermute(head, axis, [((i + 1) % count, i) for i in range(ends)])]
  transfers between devices with their start and end apart: 4 -> 5, of which waited for: 4 -> 1; matrix products, arithmetic and copies ran while one was open for 6% -> 27% of each run, Pallas kernels for 0% -> 0%
where the time goes in v1:
time: 49.8 us; the launch traced here: 49.5 us
  starting transfers between devices  14.8 us (30%)
  blocking collectives  13.5 us (27%)
  matrix products  12.9 us (26%)
  other arithmetic  3.92 us (8%)
  local copies, waits for them, and re-layouts  2.46 us (5%)
  waiting for transfers between devices  1.57 us (3%)
    all_gather x1, blocking collectives, per_device(): token_block = lax.all_gather(patches, 'rows', axis=1, tiled=True)  13.5 us
    ppermute x2, starting transfers between devices, summed_over(): lax.ppermute(values, axis, [(i, i ^ step) for i in range(count)])  7.07 us
    ppermute x1, starting transfers between devices, with_halo(): lax.ppermute(tail, axis, [(i, (i + 1) % count) for i in range(ends)])  4.97 us
    dot_general x1, matrix products, per_device(): jnp.dot(jnp.concatenate([*halves(scaled), shift[None]], axis=0), qkv_weig...  3.81 us
    dot_general x9, matrix products, per_device(): jnp.dot(window, spatial_weight[tap_row, tap_col], preferred_element_type=...  3.38 us
    dot_general x1, matrix products, per_device(): jnp.dot(jnp.concatenate([block, block], axis=1), jnp.concatenate(halves(f...  2.45 us
    ppermute x1, waiting for transfers between devices, with_halo(): lax.ppermute(head, axis, [((i + 1) % count, i) for i in range(ends)])  1.56 us
    ppermute x1, starting transfers between devices, passed_along(): return lax.ppermute(block, axis, route)  1.45 us
  transfers between devices with their start and end apart: 5, of which 1 were waited for; matrix products, arithmetic and copies ran while one was open for 27% of the time, Pallas kernels for 0%

profile of v1, /device:TPU:0, one launch (start us, length us, event | category | flops | bytes accessed | tf_op | source)
XLA Modules:
  0.0 49.5 jit_solution(3732415757868189775)
XLA Ops:
  0.0 1.2 %multiply_reduce_fusion.2 = f32[2,2,96]{2,1,0:T(2,128)S(1)} fusion(bf16[2,2,96,512]{3,2,1,0:T(8,128)(2,1)} %param.8), kind=kLoop, calls=%fused_computation.34 | loop fusion | flops 589440 | bytes 394752 | tf_op jit(solution)/shard_map/reduce_sum | solution.py:51
  1.2 1.3 %multiply_convert_fusion.2 = bf16[2,2,96,512]{3,2,1,0:T(8,128)(2,1)S(1)} fusion(f32[2,2,96]{2,1,0:T(2,128)S(1)} %add_rsqrt_fusion.3, bf16[2,2,96,512]{3,2,1,0:T(8,128)(2,1)} %param.8), kind=kLoop, calls=%fused_computation.33 | loop fusion | flops 1376256 | bytes 787968 | tf_op jit(solution)/shard_map/convert_element_type | solution.py:85
  2.6 5.0 %collective-permute-start = (bf16[2,1,96,512]{3,2,1,0:T(8,128)(2,1)S(1)}, bf16[2,1,96,512]{3,2,1,0:T(8,128)(2,1)S(1)}, u32[]{:S(2)}, u32[]{:S(2)}) collective-permute-start(bf16[2,1,96,512]{3,2,1,0:T(8,128)(2,1)S(1)} %get-tuple-element.17), channel_id=1, source_target_pairs={{0,1},{1,2},{2,3},{4,5},{5,6},{6,7},{8,9},{9,10},{10,11},{12,13},{... | collective-permute-start | bytes 589832 | tf_op jit(solution)/shard_map/ppermute | solution.py:19
  7.5 1.3 %collective-permute-start.1 = (bf16[2,1,96,512]{3,2,1,0:T(8,128)(2,1)S(1)}, bf16[2,1,96,512]{3,2,1,0:T(8,128)(2,1)S(1)}, u32[]{:S(2)}, u32[]{:S(2)}) collective-permute-start(bf16[2,1,96,512]{3,2,1,0:T(8,128)(2,1)S(1)} %get-tuple-element.18), channel_id=1, source_target_pairs={{1,0},{2,1},{3,2},{5,4},{6,5},{7,6},{9,8},{10,9},{11,10},{13,12},{... | collective-permute-start | bytes 589832 | tf_op jit(solution)/shard_map/ppermute | solution.py:21
  9.3 0.8 %dynamic_slice.7 = bf16[1280]{0:T(1024)(128)(2,1)S(1)} dynamic-slice(bf16[5120]{0:T(1024)(128)(2,1)} %param.14, s32[]{:T(128)S(6)} %select_n.4), dynamic_slice_sizes={1280} | dynamic-slice | bytes 5124 | tf_op jit(solution)/shard_map/dynamic_slice | solution.py:76
  10.2 3.8 %fusion.42 = f32[129,2304]{1,0:T(8,128)S(1)} fusion(bf16[1280,2304]{1,0:T(8,128)(2,1)} %param.15, bf16[1,1280]{1,0:T(2,128)(2,1)S(1)} %broadcast_in_dim.2, bf16[64,1280]{1,0:T(8,128)(2,1)S(1)} %get-tuple-element.6, bf16[64,1280]{1,0:T(8,128)(2,1)S(1)} %get-tuple-element.5), kind=kOutput, calls=%fused_computation.74 | convolution fusion | flops 761863680 | bytes 7417344 | tf_op jit(solution)/shard_map/dot_general | solution.py:77
  14.2 1.6 %collective-permute-done.1 = bf16[2,1,96,512]{3,2,1,0:T(8,128)(2,1)S(1)} collective-permute-done((bf16[2,1,96,512]{3,2,1,0:T(8,128)(2,1)S(1)}, bf16[2,1,96,512]{3,2,1,0:T(8,128)(2,1)S(1)}, u32[]{:S(2)}, u32[]{:S(2)}) %collective-permute-start.1) | collective-permute-done | bytes 196640 | tf_op jit(solution)/shard_map/ppermute | solution.py:21
  16.8 0.4 fusion.19
  17.2 0.4 convolution_add_fusion.7
  17.6 0.4 convolution_add_fusion.6
  17.9 0.4 convolution_add_fusion.5
  18.3 0.4 convolution_add_fusion.4
  18.7 0.4 convolution_add_fusion.3
  19.1 0.4 convolution_add_fusion.2
  19.4 0.5 multiply_reduce_fusion.1
  20.2 1.4 %collective-permute-start.2 = (bf16[2,2,96,512]{3,2,1,0:T(8,128)(2,1)S(1)}, bf16[2,2,96,512]{3,2,1,0:T(8,128)(2,1)S(1)}, u32[]{:S(2)}, u32[]{:S(2)}) collective-permute-start(bf16[2,2,96,512]{3,2,1,0:T(8,128)(2,1)S(1)} %bitcast.80), channel_id=1, source_target_pairs={{0,4},{4,8},{8,12},{1,5},{5,9},{9,13},{2,6},{6,10},{10,14},{3,7},{... | collective-permute-start | bytes 1179656 | tf_op jit(solution)/shard_map/ppermute | solution.py:31
  21.7 1.4 %convolution_multiply_fusion.2 = f32[64,64]{1,0:T(8,128)S(1)} fusion(bf16[64,5120]{1,0:T(8,128)(2,1)S(1)} %copy-done.2, f32[64]{0:T(128)S(1)} %broadcast_multiply_fusion), kind=kOutput, calls=%fused_computation.20 | convolution fusion | flops 252317696 | bytes 672000 | tf_op jit(solution)/shard_map/dot_general | solution.py:70
  23.5 0.4 fusion.16
  23.9 0.6 %copy-done.1 = bf16[2,2,96,512]{3,2,1,0:T(8,128)(2,1)S(1)} copy-done((bf16[2,2,96,512]{3,2,1,0:T(8,128)(2,1)S(1)}, bf16[2,2,96,512]{3,2,1,0:T(8,128)(2,1)}, u32[]{:S(2)}) %copy-start.1) | copy-done | bytes 393240
  24.5 0.5 %multiply_reduce_fusion = (f32[384]{0:T(512)S(1)}, f32[384,512]{1,0:T(8,128)S(1)}) fusion(f32[384,512]{1,0:T(8,128)S(1)} %fusion.14, f32[384,512]{1,0:T(8,128)S(1)} %fusion.16, bf16[384,512]{1,0:T(8,128)(2,1)S(1)} %bitcast.86, bf16[3,512,512]{2,1,0:T(8,128)(2,1)S(1)} %copy-done.3, bf16[384,512]{1,0:T(8,128)(2,1)S(1)} %bitcast.79), kind=kOutput, calls=%fused_computation.30 | convolution fusion | flops 202505856 | bytes 3671552 | tf_op jit(solution)/shard_map/dot_general | solution.py:104
  25.1 7.0 %collective-permute-start.4 = (f32[65,2304]{1,0:T(8,128)S(1)}, f32[65,2304]{1,0:T(8,128)S(1)}, u32[]{:S(2)}, u32[]{:S(2)}) collective-permute-start(f32[65,2304]{1,0:T(8,128)S(1)} %fusion.55), channel_id=1, source_target_pairs={{0,8},{4,12},{8,0},{12,4},{1,9},{5,13},{9,1},{13,5},{2,10},{6,14},... | collective-permute-start | bytes 1797128 | tf_op jit(solution)/shard_map/ppermute | solution.py:45
  32.1 0.4 convolution_convert_fusion
  32.9 13.5 %all_gather.3 = bf16[2,4,48,64]{3,2,0,1:T(8,128)(2,1)S(1)} all-gather(bf16[2,1,48,64]{3,2,0,1:T(8,128)(2,1)S(1)} %copy.14), channel_id=1, replica_groups=mesh['groups'=2,'tm'=4,'rows'=4] {'rows'}, dimensions={1}, use_global_device_ids=true | all-gather | bytes 61440 | tf_op jit(solution)/shard_map/all_gather | solution.py:117
  47.1 2.5 %broadcast_add_fusion = f32[384,2304]{1,0:T(8,128)} fusion(f32[2304]{0:T(1024)S(1)} %slice_reduce_fusion, f32[384]{0:T(512)S(1)} %add_rsqrt_fusion, bf16[64,2304]{1,0:T(8,128)(2,1)S(1)} %get-tuple-element.14, bf16[64,2304]{1,0:T(8,128)(2,1)S(1)} %get-tuple-element.13, bf16[384,64]{0,1:T(8,128)(2,1)S(1)} %reshape.100), kind=kOutput, calls=%fused_computation.3 | convolution fusion | flops 229638144 | bytes 4188672 | tf_op jit(solution)/shard_map/dot_general | solution.py:124
  (51 shorter events, 3.6 us)
Async XLA Ops:
  0.0 32.1 %copy-start = (bf16[512,16]{0,1:T(8,128)(2,1)S(1)}, bf16[512,16]{0,1:T(8,128)(2,1)}, u32[]{:S(2)}) copy-start(bf16[512,16]{0,1:T(8,128)(2,1)} %param.11) | copy-start | bytes 49156
  0.0 8.8 %copy-start.2 = (bf16[64,5120]{1,0:T(8,128)(2,1)S(1)}, bf16[64,5120]{1,0:T(8,128)(2,1)}, u32[]{:S(2)}) copy-start(bf16[64,5120]{1,0:T(8,128)(2,1)} %param.12) | copy-start | bytes 1966084
  0.0 9.1 %copy-start.4 = (bf16[5120]{0:T(1024)(128)(2,1)S(1)}, bf16[5120]{0:T(1024)(128)(2,1)}, u32[]{:S(2)}) copy-start(bf16[5120]{0:T(1024)(128)(2,1)} %param.13) | copy-start | bytes 30724
  2.6 11.7 %collective-permute-start = (bf16[2,1,96,512]{3,2,1,0:T(8,128)(2,1)S(1)}, bf16[2,1,96,512]{3,2,1,0:T(8,128)(2,1)S(1)}, u32[]{:S(2)}, u32[]{:S(2)}) collective-permute-start(bf16[2,1,96,512]{3,2,1,0:T(8,128)(2,1)S(1)} %get-tuple-element.17), channel_id=1, source_target_pairs={{0,1},{1,2},{2,3},{4,5},{5,6},{6,7},{8,9},{9,10},{10,11},{12,13},{... | collective-permute-start | bytes 589832 | tf_op jit(solution)/shard_map/ppermute | solution.py:19
  7.5 8.3 %collective-permute-start.1 = (bf16[2,1,96,512]{3,2,1,0:T(8,128)(2,1)S(1)}, bf16[2,1,96,512]{3,2,1,0:T(8,128)(2,1)S(1)}, u32[]{:S(2)}, u32[]{:S(2)}) collective-permute-start(bf16[2,1,96,512]{3,2,1,0:T(8,128)(2,1)S(1)} %get-tuple-element.18), channel_id=1, source_target_pairs={{1,0},{2,1},{3,2},{5,4},{6,5},{7,6},{9,8},{10,9},{11,10},{13,12},{... | collective-permute-start | bytes 589832 | tf_op jit(solution)/shard_map/ppermute | solution.py:21
  10.1 6.2 %slice-start = ((s8[4718592]{0:T(1024)(128)(4,1)}), s8[4194304]{0:T(1024)(128)(4,1)S(1)}, s32[]{:S(2)}) async-start(s8[4718592]{0:T(1024)(128)(4,1)} %bitcast.77), calls=%async_computation | async-start | bytes 8388608
  10.2 6.2 %slice-start.1 = ((s8[4718592]{0:T(1024)(128)(4,1)}), s8[524288]{0:T(1024)(128)(4,1)S(1)}, s32[]{:S(2)}) async-start(s8[4718592]{0:T(1024)(128)(4,1)} %bitcast.77), calls=%async_computation.1 | async-start | bytes 1048576
  14.2 10.8 %collective-permute-start.3 = (f32[65,2304]{1,0:T(8,128)S(1)}, f32[65,2304]{1,0:T(8,128)S(1)}, u32[]{:S(2)}, u32[]{:S(2)}) collective-permute-start(f32[65,2304]{1,0:T(8,128)S(1)} %pad_maximum_fusion), channel_id=1, source_target_pairs={{0,4},{4,0},{8,12},{12,8},{1,5},{5,1},{9,13},{13,9},{2,6},{6,2},{1... | collective-permute-start | bytes 1797128 | tf_op jit(solution)/shard_map/ppermute | solution.py:45
  19.9 3.2 %copy-start.3 = (bf16[3,512,512]{2,1,0:T(8,128)(2,1)S(1)}, bf16[3,512,512]{2,1,0:T(8,128)(2,1)}, u32[]{:S(2)}) copy-start(bf16[3,512,512]{2,1,0:T(8,128)(2,1)} %param.10) | copy-start | bytes 4718596
  20.2 3.3 %collective-permute-start.2 = (bf16[2,2,96,512]{3,2,1,0:T(8,128)(2,1)S(1)}, bf16[2,2,96,512]{3,2,1,0:T(8,128)(2,1)S(1)}, u32[]{:S(2)}, u32[]{:S(2)}) collective-permute-start(bf16[2,2,96,512]{3,2,1,0:T(8,128)(2,1)S(1)} %bitcast.80), channel_id=1, source_target_pairs={{0,4},{4,8},{8,12},{1,5},{5,9},{9,13},{2,6},{6,10},{10,14},{3,7},{... | collective-permute-start | bytes 1179656 | tf_op jit(solution)/shard_map/ppermute | solution.py:31
  23.5 1.0 %copy-start.1 = (bf16[2,2,96,512]{3,2,1,0:T(8,128)(2,1)S(1)}, bf16[2,2,96,512]{3,2,1,0:T(8,128)(2,1)}, u32[]{:S(2)}) copy-start(bf16[2,2,96,512]{3,2,1,0:T(8,128)(2,1)} %param.8) | copy-start | bytes 1179652
  25.1 21.8 %collective-permute-start.4 = (f32[65,2304]{1,0:T(8,128)S(1)}, f32[65,2304]{1,0:T(8,128)S(1)}, u32[]{:S(2)}, u32[]{:S(2)}) collective-permute-start(f32[65,2304]{1,0:T(8,128)S(1)} %fusion.55), channel_id=1, source_target_pairs={{0,8},{4,12},{8,0},{12,4},{1,9},{5,13},{9,1},{13,5},{2,10},{6,14},... | collective-permute-start | bytes 1797128 | tf_op jit(solution)/shard_map/ppermute | solution.py:45

commit v2 on v1

--- a/solution.py
+++ b/solution.py
@@ -1,6 +1,10 @@
+import functools
+
 import jax
 import jax.numpy as jnp
 from jax import lax
+from jax.experimental import pallas as pl
+from jax.experimental.pallas import tpu as pltpu
 from jax.sharding import PartitionSpec as P
 
 LATENT = 16
@@ -36,15 +40,76 @@
     return high.astype(jnp.bfloat16), (values - high).astype(jnp.bfloat16)
 
 
-def summed_over(values, axis):
-    count = lax.axis_size(axis)
-    if count & (count - 1):
-        return lax.psum(values, axis)
-    step = 1
+def paired_halves(values):
+    count = lax.axis_size("tm")
+    odd = lax.rem(lax.axis_index("tm"), 2) == 1
+    width = values.shape[1] // 2
+    low, high = values[:, :width], values[:, width:]
+    beside = [(i, i ^ 1) for i in range(count)]
+    return jnp.where(odd, high, low) + lax.ppermute(jnp.where(odd, low, high), "tm", beside)
+
+
+def summed_over_pairs(kept):
+    count = lax.axis_size("tm")
+    step = 2
     while step < count:
-        values = values + lax.ppermute(values, axis, [(i, i ^ step) for i in range(count)])
+        route = [(i, i ^ step) for i in range(count)]
+        kept = kept + lax.ppermute(kept.astype(jnp.bfloat16), "tm", route).astype(jnp.float32)
         step *= 2
-    return values
+    return kept
+
+
+def both_halves(kept):
+    odd = lax.rem(lax.axis_index("tm"), 2) == 1
+    other = lax.ppermute(kept, "tm", [(i, i ^ 1) for i in range(lax.axis_size("tm"))])
+    return jnp.concatenate([jnp.where(odd, other, kept), jnp.where(odd, kept, other)], axis=1)
+
+
+def gather_kernel(count, own_ref, out_ref, held, send_sem, recv_sem):
+    me = lax.axis_index("rows")
+    barrier = pltpu.get_barrier_semaphore()
+    for hop in range(1, count):
+        pl.semaphore_signal(
+            barrier,
+            inc=1,
+            device_id={"rows": lax.rem(me + hop, count)},
+            device_id_type=pl.DeviceIdType.MESH,
+        )
+    pl.semaphore_wait(barrier, count - 1)
+    copies = []
+    for hop in range(1, count):
+        copy = pltpu.make_async_remote_copy(
+            src_ref=own_ref,
+            dst_ref=held.at[hop - 1],
+            send_sem=send_sem.at[hop - 1],
+            recv_sem=recv_sem.at[hop - 1],
+            device_id={"rows": lax.rem(me + hop, count)},
+            device_id_type=pl.DeviceIdType.MESH,
+        )
+        copy.start()
+        copies.append(copy)
+    out_ref[:, me] = own_ref[...]
+    for hop in range(1, count):
+        copies[hop - 1].wait()
+        out_ref[:, lax.rem(me - hop + count, count)] = held[hop - 1]
+
+
+def gathered(patches):
+    count = lax.axis_size("rows")
+    frames, tokens, entries = patches.shape
+    return pl.pallas_call(
+        functools.partial(gather_kernel, count),
+        out_shape=jax.ShapeDtypeStruct((frames, count, tokens, entries), patches.dtype),
+        in_specs=[pl.BlockSpec(memory_space=pltpu.VMEM)],
+        out_specs=pl.BlockSpec(memory_space=pltpu.VMEM),
+        scratch_shapes=[
+            pltpu.VMEM((count - 1, frames, tokens, entries), patches.dtype),
+            pltpu.SemaphoreType.DMA((count - 1,)),
+            pltpu.SemaphoreType.DMA((count - 1,)),
+        ],
+        compiler_params=pltpu.CompilerParams(collective_id=0, has_side_effects=True),
+        cost_estimate=pl.CostEstimate(flops=0, bytes_accessed=16_000_000, transcendentals=0),
+    )(patches)
 
 
 def norm_silu(values):
@@ -63,6 +128,8 @@
     qkv_weight,
 ):
     frames_dev, rows_dev, columns, channels = features.shape
+    activated = norm_silu(features.astype(jnp.float32)).astype(jnp.bfloat16)
+    activated, embed_weight = lax.optimization_barrier((activated, embed_weight))
     depth = qkv_weight.shape[0]
     start = lax.axis_index("tm") * depth
     wide = embed_weight.astype(jnp.float32)
@@ -79,12 +146,13 @@
         qkv_weight,
         preferred_element_type=jnp.float32,
     )
-    folded = summed_over(
-        jnp.concatenate([terms[:PDIM] + terms[PDIM : 2 * PDIM], terms[2 * PDIM :]], axis=0), "tm"
-    )
-    activated = norm_silu(features.astype(jnp.float32)).astype(jnp.bfloat16)
+    kept = paired_halves(
+        jnp.concatenate([terms[:PDIM] + terms[PDIM : 2 * PDIM], terms[2 * PDIM :]], axis=0)
+    )
     rimmed = with_halo(activated, (("rows", 1),), 1)
     padded = jnp.pad(rimmed, ((0, 0), (0, 0), (1, 1), (0, 0)))
+    padded, kept = lax.optimization_barrier((padded, kept))
+    kept = summed_over_pairs(kept)
     spatial = jnp.zeros((frames_dev * rows_dev * columns, channels), jnp.float32)
     for tap_row in range(3):
         for tap_col in range(3):
@@ -97,6 +165,7 @@
     mixed_act = (
         norm_silu(spatial).astype(jnp.bfloat16).reshape(frames_dev, rows_dev, columns, channels)
     )
+    folded = both_halves(kept)
     before = passed_along(mixed_act, "tm", 1)
     stacked = jnp.concatenate([before, mixed_act], axis=0)
     temporal = jnp.zeros((frames_dev * rows_dev * columns, channels), jnp.float32)
@@ -112,9 +181,9 @@
     ).astype(jnp.bfloat16)
     latent = latent.reshape(frames_dev, 1, PATCH, columns // PATCH, PATCH, LATENT)
     patches = jnp.transpose(latent, (0, 1, 3, 2, 4, 5)).reshape(
-        frames_dev, 1, columns // PATCH, PDIM
-    )
-    token_block = lax.all_gather(patches, "rows", axis=1, tiled=True)
+        frames_dev, columns // PATCH, PDIM
+    )
+    token_block = gathered(patches)
     block_rows = token_block.shape[0] * token_block.shape[1] * token_block.shape[2]
     block = token_block.reshape(block_rows, PDIM)
     moment = jnp.dot(

time: 49.8 us -> 56.5 us (1.13)
  blocking collectives: 13.5 us -> 0 us
  waiting for transfers between devices: 1.57 us -> 10.5 us
  Pallas kernels: 0 us -> 7.29 us
  matrix products: 12.9 us -> 15.2 us
  other arithmetic: 3.92 us -> 5.63 us
  starting transfers between devices: 14.8 us -> 13.5 us
  local copies, waits for them, and re-layouts: 2.46 us -> 3.51 us
    all_gather x1 -> x0, blocking collectives: 13.5 us -> none  [per_device(): token_block = lax.all_gather(patches, 'rows', axis=1, tiled=True)]
    pallas_call x0 -> x1, Pallas kernels: none -> 7.29 us  [gathered(): pl.pallas_call(functools.partial(gather_kernel, count), out_shape=jax.Sha...]
    ppermute x2 -> x3, waiting for transfers between devices: 0.01 us -> 4.26 us  [the longest x1 4.25 us: summed_over_pairs(): lax.ppermute(kept.astype(jnp.bfloat16), 'tm', route).astype(jnp.float32)]
    ppermute x1, waiting for transfers between devices: 1.56 us -> 4.12 us  [with_halo(): lax.ppermute(head, axis, [((i + 1) % count, i) for i in range(ends)])]
    ppermute x1, waiting for transfers between devices: 0.01 us -> 2.08 us  [with_halo(): lax.ppermute(tail, axis, [(i, (i + 1) % count) for i in range(ends)])]
    dot_general x9, matrix products: 3.38 us -> 4.76 us  [per_device(): jnp.dot(window, spatial_weight[tap_row, tap_col], preferred_element_type=...]
    reduce_sum x1, other arithmetic: 0.2 us -> 1.27 us  [per_device(): wide = wide - jnp.mean(wide, axis=1, keepdims=True)]
    dot_general x1, matrix products: 0.26 us -> 1.26 us  [per_device(): jnp.dot(block.astype(jnp.float32), gram, precision=lax.Precision.HIGHEST)]
  transfers between devices with their start and end apart: 5 -> 6, of which waited for: 1 -> 3; matrix products, arithmetic and copies ran while one was open for 27% -> 12% of each run, Pallas kernels for 0% -> 13%
where the time goes in v2:
time: 56.5 us; the launch traced here: 56 us
  matrix products  15.2 us (27%)
  starting transfers between devices  13.5 us (24%)
  waiting for transfers between devices  10.5 us (19%)
  Pallas kernels  7.29 us (13%)
  other arithmetic  5.63 us (10%)
  local copies, waits for them, and re-layouts  3.51 us (6%)
    pallas_call x1, Pallas kernels, gathered(): pl.pallas_call(functools.partial(gather_kernel, count), out_shape=jax.Sha...  7.29 us
    dot_general x9, matrix products, per_device(): jnp.dot(window, spatial_weight[tap_row, tap_col], preferred_element_type=...  4.76 us
    ppermute x1, starting transfers between devices, with_halo(): lax.ppermute(tail, axis, [(i, (i + 1) % count) for i in range(ends)])  4.49 us
    ppermute x1, waiting for transfers between devices, summed_over_pairs(): lax.ppermute(kept.astype(jnp.bfloat16), 'tm', route).astype(jnp.float32)  4.25 us
    ppermute x1, waiting for transfers between devices, with_halo(): lax.ppermute(head, axis, [((i + 1) % count, i) for i in range(ends)])  4.12 us
    ppermute x1, starting transfers between devices, both_halves(): lax.ppermute(kept, 'tm', [(i, i ^ 1) for i in range(lax.axis_size('tm'))])  3.69 us
    dot_general x1, matrix products, per_device(): jnp.dot(jnp.concatenate([*halves(scaled), shift[None]], axis=0), qkv_weig...  3.66 us
    dot_general x1, matrix products, per_device(): jnp.dot(jnp.concatenate([block, block], axis=1), jnp.concatenate(halves(f...  2.47 us
  transfers between devices with their start and end apart: 6, of which 3 were waited for; matrix products, arithmetic and copies ran while one was open for 12% of the time, Pallas kernels for 13%

profile of v2, /device:TPU:0, one launch (start us, length us, event | category | flops | bytes accessed | tf_op | source)
XLA Modules:
  0.0 56.0 jit_solution(2312017624414245407)
XLA Ops:
  0.0 0.8 %convert_add_fusion.1 = f32[5120]{0:T(1024)S(1)} fusion(bf16[5120]{0:T(1024)(128)(2,1)} %param.13), kind=kLoop, calls=%fused_computation.93 | loop fusion | flops 10240 | bytes 30720 | tf_op jit(solution)/shard_map/add | solution.py:141
  0.8 1.2 %multiply_reduce_fusion.2 = f32[2,2,96]{2,1,0:T(2,128)S(1)} fusion(bf16[2,2,96,512]{3,2,1,0:T(8,128)(2,1)} %param.8), kind=kLoop, calls=%fused_computation.34 | loop fusion | flops 589440 | bytes 394752 | tf_op jit(solution)/shard_map/reduce_sum | solution.py:116
  2.0 1.3 %multiply_convert_fusion.2 = bf16[2,2,96,512]{3,2,1,0:T(8,128)(2,1)S(1)} fusion(f32[2,2,96]{2,1,0:T(2,128)S(1)} %add_rsqrt_fusion.3, bf16[2,2,96,512]{3,2,1,0:T(8,128)(2,1)} %param.8), kind=kLoop, calls=%fused_computation.33 | loop fusion | flops 1376256 | bytes 787968 | tf_op jit(solution)/shard_map/convert_element_type | solution.py:131
  3.2 1.3 %convert_reduce_fusion = f32[64]{0:T(128)S(1)} fusion(bf16[64,5120]{1,0:T(8,128)(2,1)} %param.12), kind=kLoop, calls=%fused_computation.6 | loop fusion | flops 655296 | bytes 655616 | tf_op jit(solution)/shard_map/reduce_sum | solution.py:136
  4.8 0.8 %dynamic_slice.7 = bf16[1280]{0:T(1024)(128)(2,1)S(1)} dynamic-slice(bf16[5120]{0:T(1024)(128)(2,1)} %param.14, s32[]{:T(128)S(6)} %select_n.25), dynamic_slice_sizes={1280} | dynamic-slice | bytes 5124 | tf_op jit(solution)/shard_map/dynamic_slice | solution.py:143
  5.6 3.7 %fusion.41 = f32[129,2304]{1,0:T(8,128)S(1)} fusion(bf16[1280,2304]{1,0:T(8,128)(2,1)} %param.15, bf16[1,1280]{1,0:T(2,128)(2,1)S(1)} %broadcast_in_dim.2, bf16[64,1280]{1,0:T(8,128)(2,1)S(1)} %get-tuple-element.14, bf16[64,1280]{1,0:T(8,128)(2,1)S(1)} %get-tuple-element.13), kind=kOutput, calls=%fused_computation.75 | convolution fusion | flops 761863680 | bytes 7417344 | tf_op jit(solution)/shard_map/dot_general | solution.py:144
  9.4 0.6 collective-permute-start.2
  10.0 4.5 %collective-permute-start = (bf16[2,1,96,512]{3,2,1,0:T(8,128)(2,1)S(1)}, bf16[2,1,96,512]{3,2,1,0:T(8,128)(2,1)S(1)}, u32[]{:S(2)}, u32[]{:S(2)}) collective-permute-start(bf16[2,1,96,512]{3,2,1,0:T(8,128)(2,1)S(1)} %get-tuple-element.28), channel_id=1, source_target_pairs={{0,1},{1,2},{2,3},{4,5},{5,6},{6,7},{8,9},{9,10},{10,11},{12,13},{... | collective-permute-start | bytes 589832 | tf_op jit(solution)/shard_map/ppermute | solution.py:23
  14.5 1.3 %collective-permute-start.1 = (bf16[2,1,96,512]{3,2,1,0:T(8,128)(2,1)S(1)}, bf16[2,1,96,512]{3,2,1,0:T(8,128)(2,1)S(1)}, u32[]{:S(2)}, u32[]{:S(2)}) collective-permute-start(bf16[2,1,96,512]{3,2,1,0:T(8,128)(2,1)S(1)} %get-tuple-element.29), channel_id=1, source_target_pairs={{1,0},{2,1},{3,2},{5,4},{6,5},{7,6},{9,8},{10,9},{11,10},{13,12},{... | collective-permute-start | bytes 589832 | tf_op jit(solution)/shard_map/ppermute | solution.py:25
  15.8 1.4 %convolution_multiply_fusion.2 = f32[64,64]{1,0:T(8,128)S(1)} fusion(bf16[64,5120]{1,0:T(8,128)(2,1)S(1)} %copy-done.2, f32[64]{0:T(128)S(1)} %broadcast_multiply_fusion), kind=kOutput, calls=%fused_computation.20 | convolution fusion | flops 252317696 | bytes 672000 | tf_op jit(solution)/shard_map/dot_general | solution.py:137
  17.2 2.1 %collective-permute-done = bf16[2,1,96,512]{3,2,1,0:T(8,128)(2,1)S(1)} collective-permute-done((bf16[2,1,96,512]{3,2,1,0:T(8,128)(2,1)S(1)}, bf16[2,1,96,512]{3,2,1,0:T(8,128)(2,1)S(1)}, u32[]{:S(2)}, u32[]{:S(2)}) %collective-permute-start) | collective-permute-done | bytes 196640 | tf_op jit(solution)/shard_map/ppermute | solution.py:23
  19.3 4.1 %collective-permute-done.1 = bf16[2,1,96,512]{3,2,1,0:T(8,128)(2,1)S(1)} collective-permute-done((bf16[2,1,96,512]{3,2,1,0:T(8,128)(2,1)S(1)}, bf16[2,1,96,512]{3,2,1,0:T(8,128)(2,1)S(1)}, u32[]{:S(2)}, u32[]{:S(2)}) %collective-permute-start.1) | collective-permute-done | bytes 196640 | tf_op jit(solution)/shard_map/ppermute | solution.py:25
  23.7 0.5 fusion.56
  24.3 1.7 %fusion.27 = f32[384,512]{1,0:T(8,128)S(1)} fusion(bf16[384,512]{1,0:T(8,128)(2,1)S(1)} %bitcast.89, bf16[3,3,512,512]{3,2,1,0:T(8,128)(2,1)} %param.9), kind=kOutput, calls=%fused_computation.58 | convolution fusion | flops 201326592 | bytes 1703936 | tf_op jit(solution)/shard_map/dot_general | solution.py:162
  29.5 1.3 %collective-permute-start.3 = (bf16[2,2,96,512]{3,2,1,0:T(8,128)(2,1)S(1)}, bf16[2,2,96,512]{3,2,1,0:T(8,128)(2,1)S(1)}, u32[]{:S(2)}, u32[]{:S(2)}) collective-permute-start(bf16[2,2,96,512]{3,2,1,0:T(8,128)(2,1)S(1)} %bitcast.78), channel_id=1, source_target_pairs={{0,4},{4,8},{8,12},{1,5},{5,9},{9,13},{2,6},{6,10},{10,14},{3,7},{... | collective-permute-start | bytes 1179656 | tf_op jit(solution)/shard_map/ppermute | solution.py:35
  30.9 2.2 %collective-permute-start.4 = (bf16[65,1152]{1,0:T(8,128)(2,1)S(1)}, bf16[65,1152]{1,0:T(8,128)(2,1)S(1)}, u32[]{:S(2)}, u32[]{:S(2)}) collective-permute-start(bf16[65,1152]{1,0:T(8,128)(2,1)S(1)} %convert_element_type.55), channel_id=1, source_target_pairs={{0,8},{4,12},{8,0},{12,4},{1,9},{5,13},{9,1},{13,5},{2,10},{6,14},... | collective-permute-start | bytes 449288 | tf_op jit(solution)/shard_map/ppermute | solution.py:57
  33.5 4.3 %collective-permute-done.4 = bf16[65,1152]{1,0:T(8,128)(2,1)S(1)} collective-permute-done((bf16[65,1152]{1,0:T(8,128)(2,1)S(1)}, bf16[65,1152]{1,0:T(8,128)(2,1)S(1)}, u32[]{:S(2)}, u32[]{:S(2)}) %collective-permute-start.4) | collective-permute-done | bytes 149792 | tf_op jit(solution)/shard_map/ppermute | solution.py:57
  37.8 3.7 %collective-permute-start.5 = (f32[65,1152]{1,0:T(8,128)S(1)}, f32[65,1152]{1,0:T(8,128)S(1)}, u32[]{:S(2)}, u32[]{:S(2)}) collective-permute-start(f32[65,1152]{1,0:T(8,128)S(1)} %convert_add_fusion), channel_id=1, source_target_pairs={{0,4},{4,0},{8,12},{12,8},{1,5},{5,1},{9,13},{13,9},{2,6},{6,2},{1... | collective-permute-start | bytes 898568 | tf_op jit(solution)/shard_map/ppermute | solution.py:64
  41.9 0.5 multiply_reduce_fusion
  43.1 0.7 %copy.13.own_ref = bf16[2,48,64]{2,1,0:T(8,128)(2,1)} copy(bf16[2,48,64]{1,2,0:T(8,128)(2,1)S(1)} %bitcast.95) | data formatting | bytes 24576 | tf_op jit(solution)/shard_map/reshape | solution.py:183
  43.8 7.3 %shard_map.82 = bf16[2,4,48,64]{3,2,1,0:T(8,128)(2,1)} custom-call(bf16[2,48,64]{2,1,0:T(8,128)(2,1)} %copy.13.own_ref), custom_call_target="tpu_custom_call" | custom-call | bytes 16000000 | tf_op jit(solution)/shard_map/pallas_call | solution.py:100
  51.1 1.0 %copy.14 = bf16[384,64]{0,1:T(8,128)(2,1)S(1)} copy(bf16[384,64]{1,0:T(8,128)(2,1)} %bitcast.91) | data formatting | bytes 98304 | tf_op jit(solution)/shard_map/reshape | solution.py:188
  52.1 1.3 %fusion.3 = f32[384]{0:T(512)S(1)} fusion(bf16[384,64]{1,0:T(8,128)(2,1)} %bitcast.92, f32[64,64]{1,0:T(8,128)S(1)} %convolution_multiply_fusion.2, bf16[384,64]{0,1:T(8,128)(2,1)S(1)} %copy.14), kind=kOutput, calls=%fused_computation.19 | convolution fusion | flops 18947712 | bytes 116224 | tf_op jit(solution)/shard_map/dot_general | solution.py:189
  53.5 2.5 %broadcast_add_fusion = f32[384,2304]{1,0:T(8,128)} fusion(f32[2304]{0:T(1024)S(1)} %fusion.52, f32[384]{0:T(512)S(1)} %add_rsqrt_fusion, bf16[64,2304]{1,0:T(8,128)(2,1)S(1)} %get-tuple-element.25, bf16[64,2304]{1,0:T(8,128)(2,1)S(1)} %get-tuple-element.24, bf16[384,64]{1,0:T(8,128)(2,1)S(1)} %bitcast.93), kind=kOutput, calls=%fused_computation.3 | convolution fusion | flops 229638144 | bytes 4188672 | tf_op jit(solution)/shard_map/dot_general | solution.py:193
  (53 shorter events, 5.9 us)
Async XLA Ops:
  0.0 42.4 %copy-start = (bf16[512,16]{0,1:T(8,128)(2,1)S(1)}, bf16[512,16]{0,1:T(8,128)(2,1)}, u32[]{:S(2)}) copy-start(bf16[512,16]{0,1:T(8,128)(2,1)} %param.11) | copy-start | bytes 49156
  0.0 4.5 %copy-start.2 = (bf16[64,5120]{1,0:T(8,128)(2,1)S(1)}, bf16[64,5120]{1,0:T(8,128)(2,1)}, u32[]{:S(2)}) copy-start(bf16[64,5120]{1,0:T(8,128)(2,1)} %param.12) | copy-start | bytes 1966084
  9.4 14.2 %collective-permute-start.2 = (f32[65,1152]{1,0:T(8,128)S(1)}, f32[65,1152]{1,0:T(8,128)S(1)}, u32[]{:S(2)}, u32[]{:S(2)}) collective-permute-start(f32[65,1152]{1,0:T(8,128)S(1)} %broadcast_select_fusion.2), channel_id=1, source_target_pairs={{0,4},{4,0},{8,12},{12,8},{1,5},{5,1},{9,13},{13,9},{2,6},{6,2},{1... | collective-permute-start | bytes 898568 | tf_op jit(solution)/shard_map/ppermute | solution.py:49
  10.0 9.3 %collective-permute-start = (bf16[2,1,96,512]{3,2,1,0:T(8,128)(2,1)S(1)}, bf16[2,1,96,512]{3,2,1,0:T(8,128)(2,1)S(1)}, u32[]{:S(2)}, u32[]{:S(2)}) collective-permute-start(bf16[2,1,96,512]{3,2,1,0:T(8,128)(2,1)S(1)} %get-tuple-element.28), channel_id=1, source_target_pairs={{0,1},{1,2},{2,3},{4,5},{5,6},{6,7},{8,9},{9,10},{10,11},{12,13},{... | collective-permute-start | bytes 589832 | tf_op jit(solution)/shard_map/ppermute | solution.py:23
  14.5 8.9 %collective-permute-start.1 = (bf16[2,1,96,512]{3,2,1,0:T(8,128)(2,1)S(1)}, bf16[2,1,96,512]{3,2,1,0:T(8,128)(2,1)S(1)}, u32[]{:S(2)}, u32[]{:S(2)}) collective-permute-start(bf16[2,1,96,512]{3,2,1,0:T(8,128)(2,1)S(1)} %get-tuple-element.29), channel_id=1, source_target_pairs={{1,0},{2,1},{3,2},{5,4},{6,5},{7,6},{9,8},{10,9},{11,10},{13,12},{... | collective-permute-start | bytes 589832 | tf_op jit(solution)/shard_map/ppermute | solution.py:25
  23.6 2.4 %slice-start = ((s8[4718592]{0:T(1024)(128)(4,1)}), s8[4194304]{0:T(1024)(128)(4,1)S(1)}, s32[]{:S(2)}) async-start(s8[4718592]{0:T(1024)(128)(4,1)} %bitcast.75), calls=%async_computation | async-start | bytes 8388608
  23.7 2.4 %slice-start.1 = ((s8[4718592]{0:T(1024)(128)(4,1)}), s8[524288]{0:T(1024)(128)(4,1)S(1)}, s32[]{:S(2)}) async-start(s8[4718592]{0:T(1024)(128)(4,1)} %bitcast.75), calls=%async_computation.1 | async-start | bytes 1048576
  28.8 4.3 %copy-start.3 = (bf16[3,512,512]{2,1,0:T(8,128)(2,1)S(1)}, bf16[3,512,512]{2,1,0:T(8,128)(2,1)}, u32[]{:S(2)}) copy-start(bf16[3,512,512]{2,1,0:T(8,128)(2,1)} %param.10) | copy-start | bytes 4718596
  29.5 11.9 %collective-permute-start.3 = (bf16[2,2,96,512]{3,2,1,0:T(8,128)(2,1)S(1)}, bf16[2,2,96,512]{3,2,1,0:T(8,128)(2,1)S(1)}, u32[]{:S(2)}, u32[]{:S(2)}) collective-permute-start(bf16[2,2,96,512]{3,2,1,0:T(8,128)(2,1)S(1)} %bitcast.78), channel_id=1, source_target_pairs={{0,4},{4,8},{8,12},{1,5},{5,9},{9,13},{2,6},{6,10},{10,14},{3,7},{... | collective-permute-start | bytes 1179656 | tf_op jit(solution)/shard_map/ppermute | solution.py:35
  30.9 6.8 %collective-permute-start.4 = (bf16[65,1152]{1,0:T(8,128)(2,1)S(1)}, bf16[65,1152]{1,0:T(8,128)(2,1)S(1)}, u32[]{:S(2)}, u32[]{:S(2)}) collective-permute-start(bf16[65,1152]{1,0:T(8,128)(2,1)S(1)} %convert_element_type.55), channel_id=1, source_target_pairs={{0,8},{4,12},{8,0},{12,4},{1,9},{5,13},{9,1},{13,5},{2,10},{6,14},... | collective-permute-start | bytes 449288 | tf_op jit(solution)/shard_map/ppermute | solution.py:57
  33.4 8.4 %copy-start.1 = (bf16[2,2,96,512]{3,2,1,0:T(8,128)(2,1)S(1)}, bf16[2,2,96,512]{3,2,1,0:T(8,128)(2,1)}, u32[]{:S(2)}) copy-start(bf16[2,2,96,512]{3,2,1,0:T(8,128)(2,1)} %param.8) | copy-start | bytes 1179652
  37.8 15.6 %collective-permute-start.5 = (f32[65,1152]{1,0:T(8,128)S(1)}, f32[65,1152]{1,0:T(8,128)S(1)}, u32[]{:S(2)}, u32[]{:S(2)}) collective-permute-start(f32[65,1152]{1,0:T(8,128)S(1)} %convert_add_fusion), channel_id=1, source_target_pairs={{0,4},{4,0},{8,12},{12,8},{1,5},{5,1},{9,13},{13,9},{2,6},{6,2},{1... | collective-permute-start | bytes 898568 | tf_op jit(solution)/shard_map/ppermute | solution.py:64
  52.1 1.5 %copy-start.4 = (bf16[2,4,48,64]{3,2,1,0:T(8,128)(2,1)S(1)}, bf16[2,4,48,64]{3,2,1,0:T(8,128)(2,1)}, u32[]{:S(2)}) copy-start(bf16[2,4,48,64]{3,2,1,0:T(8,128)(2,1)} %shard_map.82) | copy-start | bytes 147460
